TPU v7x, 256 devices: a whole 4x4x8 slice. The times are simulated.
256 devices in a mesh: store: 16 (over z_lo, y), seq: 16 (over z_hi, x, core).
Axes of the slice: x: 4, y: 4, z: 8 (z_hi: 2, z_lo: 4; z = z_hi * 4 + z_lo), core: 2. Of those that a mesh axis runs over, the one named last changes fastest.
Arguments:
- store_kv: bfloat16 [256, 640, 2048], P('store', 'seq'), may hold values from -8 to 8
- span_len: int32 [16, 144], replicated, may hold values from 18 to 40, as said below
- span_shard: int32 [16, 16], replicated, may hold values from 0 to 15, each once within a row
- q_sel: bfloat16 [16, 1024, 8192], P('store', 'seq'), may hold values from -8 to 8
- fresh_kv: bfloat16 [16, 1024, 2048], P('store', 'seq'), may hold values from -8 to 8
- sel_pos: int32 [16, 1024], P('store', 'seq'), may hold values from -1 to 4095, as said below
Outputs:
- blended_kv: bfloat16 [16, 4096, 2048], P('store', 'seq')
- attn_out: bfloat16 [16, 1024, 8192], P('store', 'seq')
Inputs may be any that keep to these rules, and one draw needn't show every extreme that they name: `span_len`: each row sums to 4096, and its largest entry is 40. `span_shard`: each row names every store shard once. `sel_pos`: on seq index q, the 64 slots of a request hold distinct positions from q * 256 to (q + 1) * 256 - 1 in rising order, then -1 in unused slots; at least 2 slots are used, and in every draw some device uses all 64.
All inputs are finite; a program needn't handle non-finite values.
Results may differ from a plain program's by a relative error of at most 0.007.
Values may be sent and summed in bfloat16 or wider, within the bound.
No kernel may reach another device: no remote copies, remote signals or barrier semaphores. Data moves between devices by JAX's collectives and lax.ppermute only.
A program may use at most 192 MiB of HBM per device.

v0:
```python
import math
import jax
import jax.numpy as jnp
from jax import lax
from jax.sharding import PartitionSpec as P

HEADS = 64
KV_HEADS = 8
D_HEAD = 128
TOK_DEV = 256
ROPE_BASE = 500000.0


def rotate_keys(kv_rows, span_start):
    half_dim = D_HEAD // 2
    kv_width = KV_HEADS * D_HEAD
    row_count = kv_rows.shape[0]
    inverse = jnp.power(ROPE_BASE, -(jnp.arange(half_dim, dtype=jnp.float32) * 2.0 / D_HEAD))
    angles = span_start.astype(jnp.float32)[:, None] * inverse[None, :]
    cosine = jnp.cos(angles)[:, None, :]
    sine_part = jnp.sin(angles)[:, None, :]
    key_rows = kv_rows[:, :kv_width].reshape(row_count, KV_HEADS, D_HEAD)
    lower_half = key_rows[..., :half_dim]
    upper_half = key_rows[..., half_dim:]
    turned = jnp.concatenate(
        [
            lower_half * cosine - upper_half * sine_part,
            upper_half * cosine + lower_half * sine_part,
        ],
        axis=2,
    )
    return jnp.concatenate([turned.reshape(row_count, kv_width), kv_rows[:, kv_width:]], axis=1)


def locate(span_lengths, span_holders, positions):
    span_starts = jnp.cumsum(span_lengths) - span_lengths
    span_ids = jnp.arange(span_lengths.shape[0], dtype=jnp.int32)
    inside = (positions[:, None] >= span_starts[None, :]).astype(jnp.int32)
    which_span = jnp.sum(inside, axis=1) - 1
    picked = (which_span[:, None] == span_ids[None, :]).astype(jnp.int32)
    holder = jnp.sum(picked * span_holders[None, :], axis=1)
    span_start = jnp.sum(picked * span_starts[None, :], axis=1)
    return (holder, span_start)


def empty_states(row_count):
    groups = HEADS // KV_HEADS
    return (
        jnp.full((KV_HEADS, groups, row_count), -1e30, jnp.float32),
        jnp.zeros((KV_HEADS, groups, row_count), jnp.float32),
        jnp.zeros((KV_HEADS, groups, row_count, D_HEAD), jnp.float32),
    )


def absorb(states, queries, limits, kv_piece, first_row):

    def update(current):
        running_max, running_sum, weighted = current
        row_count = kv_piece.shape[0]
        kv_width = KV_HEADS * D_HEAD
        key_rows = kv_piece[:, :kv_width].reshape(row_count, KV_HEADS, D_HEAD)
        value_rows = kv_piece[:, kv_width:].reshape(row_count, KV_HEADS, D_HEAD)
        grouped = queries.reshape(queries.shape[0], KV_HEADS, HEADS // KV_HEADS, D_HEAD)
        scores = jnp.einsum(
            "qhgd,khd->hgqk", grouped, key_rows, preferred_element_type=jnp.float32
        ) / math.sqrt(D_HEAD)
        key_positions = jnp.arange(row_count, dtype=jnp.int32)
        allowed = (key_positions[None, :] <= limits[:, None])[None, None]
        piece_max = jnp.max(jnp.where(allowed, scores, -jnp.inf), axis=3)
        raised = jnp.maximum(running_max, piece_max)
        weights = jnp.where(allowed, jnp.exp(scores - raised[..., None]), 0.0)
        running_sum = jnp.sum(weights, axis=3)
        weighted = jnp.einsum(
            "hgqk,khd->hgqd",
            weights.astype(jnp.bfloat16),
            value_rows,
            preferred_element_type=jnp.float32,
        )
        return (raised, running_sum, weighted)

    useful = (first_row >= 0) & (first_row <= jnp.max(limits))
    return lax.cond(useful, update, lambda current: current, states)


def finish(states):
    running_max, running_sum, weighted = states
    normed = weighted / running_sum[..., None]
    return jnp.transpose(normed, (2, 0, 1, 3)).reshape(normed.shape[2], HEADS * D_HEAD)


def on_device(store_kv, span_len, span_shard, q_sel, fresh_kv, sel_pos):
    slot_rows = store_kv.shape[1]
    request = lax.axis_index("store")
    stripe = lax.axis_index("seq")
    fetched = lax.all_to_all(store_kv, "store", split_axis=0, concat_axis=0, tiled=True)
    lengths_row = lax.dynamic_index_in_dim(span_len, request, 0, keepdims=False)
    shards_row = lax.dynamic_index_in_dim(span_shard, request, 0, keepdims=False)
    holders_row = jnp.tile(shards_row, span_len.shape[1] // span_shard.shape[1])
    positions = stripe * TOK_DEV + jnp.arange(TOK_DEV, dtype=jnp.int32)
    holder, span_start = locate(lengths_row, holders_row, positions)
    offset = positions - jnp.maximum(span_start, stripe * TOK_DEV)
    flat_rows = fetched.reshape(-1, fetched.shape[2])
    cached = jnp.take(flat_rows, holder * slot_rows + offset, axis=0)
    rotated = rotate_keys(cached.astype(jnp.float32), span_start)
    chosen = sel_pos[0]
    matches = positions[:, None] == chosen[None, :]
    fresh_rows = jnp.dot(
        matches.astype(jnp.bfloat16), fresh_kv[0], preferred_element_type=jnp.float32
    )
    blended = jnp.where(jnp.any(matches, axis=1)[:, None], fresh_rows, rotated).astype(jnp.bfloat16)
    queries = q_sel[0]
    limits = jnp.maximum(chosen, 0)
    groups = ((queries, limits),)
    initial = tuple((empty_states(member[0].shape[0]) for member in groups))
    kv_piece = lax.all_gather(blended, "seq", axis=0, tiled=True)
    first_row = jnp.int32(0)
    finished = tuple(
        (
            absorb(member_state, member[0], member[1], kv_piece, first_row)
            for member_state, member in zip(initial, groups)
        )
    )
    attention = finish(finished[0]).astype(jnp.bfloat16)
    attended = jnp.where((chosen >= 0)[:, None], attention, jnp.zeros_like(attention))
    return (blended[None], attended[None])


def solution(mesh):
    return jax.shard_map(
        on_device,
        mesh=mesh,
        in_specs=(
            P("store", "seq", None),
            P(),
            P(),
            P("store", "seq", None),
            P("store", "seq", None),
            P("store", "seq"),
        ),
        out_specs=(P("store", "seq", None), P("store", "seq", None)),
        check_vma=False,
    )
```

profile of v0, /device:TPU:1, one launch (start us, length us, event | category | flops | bytes accessed | tf_op | source)
XLA Modules:
  0.0 371.7 jit_solution(6813124720219924720)
XLA Ops:
  7.2 9.3 %all-to-all-start = ((bf16[16,40,2048]{2,1,0:T(8,128)(2,1)}), bf16[16,40,2048]{2,1,0:T(8,128)(2,1)S(1)}, u32[]{:S(2)}, u32[]{:S(2)}) async-start(bf16[16,40,2048]{2,1,0:T(8,128)(2,1)} %param.8), calls=%async_computation | async-start | bytes 5242880 | tf_op jit(solution)/shard_map/all_to_all | solution.py:95
  16.6 0.7 constant_dynamic-slice_fusion
  17.3 0.3 reduce-window.9
  17.7 0.7 dynamic-slice_bitcast_fusion
  18.5 0.1 slice_reduce_fusion
  18.7 0.1 convert_reduce_fusion
  18.8 0.1 select_reduce_fusion
  19.0 0.7 compare_reduce_fusion
  19.8 0.5 multiply_cosine_fusion
  20.3 46.9 %all-to-all-done = bf16[16,40,2048]{2,1,0:T(8,128)(2,1)S(1)} async-done(((bf16[16,40,2048]{2,1,0:T(8,128)(2,1)}), bf16[16,40,2048]{2,1,0:T(8,128)(2,1)S(1)}, u32[]{:S(2)}, u32[]{:S(2)}) %all-to-all-start) | async-done | bytes 2621472 | tf_op jit(solution)/shard_map/all_to_all | solution.py:95
  67.2 2.3 gather_fusion
  69.5 1.4 select_convert_fusion
  70.9 0.1 slice_bitcast_fusion
  71.1 0.2 copy.28
  71.3 0.5 multiply_subtract_fusion
  71.8 0.3 pad_maximum_fusion
  72.1 0.1 copy.35
  72.3 1.5 fusion.12
  73.8 0.6 broadcast_maximum_fusion.2
  75.1 182.5 %all-gather.2.cloned.1.call-done = bf16[4096,2048]{1,0:T(8,128)(2,1)} async-done(((bf16[256,2048]{1,0:T(8,128)(2,1)}), bf16[4096,2048]{1,0:T(8,128)(2,1)}) %all-gather.2.cloned.1.call-update) | async-done | bytes 16777232 | tf_op jit(solution)/shard_map/all_gather | solution.py:115
  257.6 103.0 %conditional.1 = (f32[8,8,64]{2,1,0:T(8,128)S(1)}, f32[8,8,64,128]{3,2,1,0:T(8,128)}) conditional(s32[]{:T(128)} %convert_element_type.44, () %tuple.16, (s32[64]{0:T(128)S(1)}, bf16[4096,2048]{1,0:T(8,128)(2,1)}, bf16[1,64,8192]{2,1,0:T(8,128)(2,1)}) %tuple.17), branch_computations={%region_7.8_spmd, %region_8.11_spmd} | conditional | flops 8774742016 | bytes 295797056 | solution.py:82
  257.6 0.2 iota_compare_fusion
  257.8 20.7 %copy.19 = bf16[4096,2048]{0,1:T(8,128)(2,1)} copy(bf16[4096,2048]{1,0:T(8,128)(2,1)} %get-tuple-element.21) | data formatting | bytes 33554432 | tf_op jit(solution)/shard_map
  278.5 9.5 %fusion.19 = (bf16[4096,1024]{0,1:T(8,128)(2,1)}, bf16[4096,1024]{0,1:T(8,128)(2,1)S(1)}) fusion(bf16[4096,2048]{0,1:T(8,128)(2,1)} %copy.19), kind=kLoop, calls=%fused_computation.56 | loop fusion | bytes 33554432 | tf_op jit(solution)/shard_map/cond/branch_1_fun/slice | solution.py:62
  288.0 0.3 copy.27
  288.3 23.6 %fusion = (f32[8,8,64]{2,1,0:T(8,128)S(1)}, f32[8,4096,64,8]{1,2,3,0:T(8,128)}) fusion(pred[64,4096]{1,0:T(8,128)(4,1)S(1)} %iota_compare_fusion, bf16[4096,8,128,1]{0,2,3,1:T(8,128)(2,1)S(1)} %bitcast.62, bf16[64,8,8,128]{3,2,1,0:T(8,128)(2,1)S(1)} %bitcast.65), kind=kOutput, calls=%fused_computation.3 | convolution fusion | flops 4345294848 | bytes 76824576 | tf_op jit(solution)/shard_map/cond/branch_1_fun/qhgd,khd->hgqk/dot_general | solution.py:64
  311.9 27.0 %fusion.5 = f32[8,8,64,128]{3,2,1,0:T(8,128)} fusion(bf16[4096,8,128,1]{0,2,3,1:T(8,128)(2,1)} %bitcast.64, f32[8,4096,64,8]{1,2,3,0:T(8,128)} %get-tuple-element.30, f32[8,8,64]{2,1,0:T(8,128)S(1)} %broadcast_maximum_fusion, pred[64,4096]{1,0:T(8,128)(4,1)S(1)} %iota_compare_fusion), kind=kOutput, calls=%fused_computation.8 | convolution fusion | flops 4362076160 | bytes 77873152 | tf_op jit(solution)/shard_map/cond/branch_1_fun/hgqk,khd->hgqd/dot_general | solution.py:73
  338.9 21.6 %fusion.4 = f32[8,8,64]{2,1,0:T(8,128)S(1)} fusion(f32[8,4096,64,8]{1,2,3,0:T(8,128)} %get-tuple-element.30, f32[8,8,64]{2,1,0:T(8,128)S(1)} %broadcast_maximum_fusion, pred[64,4096]{1,0:T(8,128)(4,1)S(1)} %iota_compare_fusion), kind=kLoop, calls=%fused_computation.7 | loop fusion | flops 67104768 | bytes 67403776 | tf_op jit(solution)/shard_map/cond/branch_1_fun/reduce_sum | solution.py:72
  360.6 2.0 fusion.13
  362.6 0.7 copy.20
  363.3 0.5 convert_element_type.47
  363.8 1.1 broadcast_select_fusion
  (28 shorter events, 0.5 us)
Async XLA Ops:
  7.2 65.1 %copy-start = (bf16[1,64,2048]{2,1,0:T(8,128)(2,1)S(1)}, bf16[1,64,2048]{2,1,0:T(8,128)(2,1)}, u32[]{:S(2)}) copy-start(bf16[1,64,2048]{2,1,0:T(8,128)(2,1)} %param.12) | copy-start | bytes 786436
  7.2 65.1 %copy-start.3 = (s32[1,64]{1,0:T(1,128)S(1)}, s32[1,64]{1,0:T(1,128)}, u32[]{:S(2)}) copy-start(s32[1,64]{1,0:T(1,128)} %param.13) | copy-start | bytes 772
  7.2 60.0 %all-to-all-start = ((bf16[16,40,2048]{2,1,0:T(8,128)(2,1)}), bf16[16,40,2048]{2,1,0:T(8,128)(2,1)S(1)}, u32[]{:S(2)}, u32[]{:S(2)}) async-start(bf16[16,40,2048]{2,1,0:T(8,128)(2,1)} %param.8), calls=%async_computation | async-start | bytes 5242880 | tf_op jit(solution)/shard_map/all_to_all | solution.py:95
  16.5 241.0 %all-gather.2.cloned.1.call-start = ((), (), s32[]{:S(2)}) async-start(), calls=%async_computation.1 | async-start | bytes 17825792 | tf_op jit(solution)/shard_map/all_gather | solution.py:115
  278.5 9.5 %copy-start.2 = (bf16[1,64,8192]{2,1,0:T(8,128)(2,1)S(1)}, bf16[1,64,8192]{2,1,0:T(8,128)(2,1)}, u32[]{:S(2)}) copy-start(bf16[1,64,8192]{2,1,0:T(8,128)(2,1)} %get-tuple-element.16) | copy-start | bytes 3145732 | tf_op jit(solution)/shard_map/cond
  360.6 4.3 %copy-start.1 = (bf16[1,64,2048]{2,1,0:T(8,128)(2,1)S(1)}, bf16[1,64,2048]{2,1,0:T(8,128)(2,1)}, u32[]{:S(2)}) copy-start(bf16[1,64,2048]{2,1,0:T(8,128)(2,1)} %param.12) | copy-start | bytes 786436
Sparse Core Ops, SparseCore 0:
  73.9 183.5 all-gather.1
where the time goes:
time: 373 us; the launch traced here: 372 us
  waiting for transfers between devices  229 us (61%)
  matrix products  52.2 us (14%)
  local copies, waits for them, and re-layouts  36.2 us (10%)
  other arithmetic  29.8 us (8%)
  between operations  14.9 us (4%)
  starting transfers between devices  9.36 us (3%)
    all_gather x1, waiting for transfers between devices, on_device(): kv_piece = lax.all_gather(blended, 'seq', axis=0, tiled=True)  182 us
    all_to_all x1, waiting for transfers between devices, on_device(): lax.all_to_all(store_kv, 'store', split_axis=0, concat_axis=0, tiled=True)  46.9 us
    dot_general x1, matrix products, update(): jnp.einsum('hgqk,khd->hgqd', weights.astype(jnp.bfloat16), value_rows, pr...  27 us
    dot_general x1, matrix products, update(): jnp.einsum('qhgd,khd->hgqk', grouped, key_rows, preferred_element_type=jn...  23.6 us
    reduce_sum x1, other arithmetic, update(): running_sum = jnp.sum(weights, axis=3)  21.6 us
    another operation x2, local copies, waits for them, and re-layouts  20.9 us
    slice x1, local copies, waits for them, and re-layouts, update(): value_rows = kv_piece[:, kv_width:].reshape(row_count, KV_HEADS, D_HEAD)  9.49 us
    all_to_all x1, starting transfers between devices, on_device(): lax.all_to_all(store_kv, 'store', split_axis=0, concat_axis=0, tiled=True)  9.32 us
  transfers between devices with their start and end apart: 2, of which 2 were waited for; matrix products, arithmetic and copies ran while one was open for 1% of the time, Pallas kernels for 0%

commit v1 on v0

--- a/solution.py
+++ b/solution.py
@@ -112,7 +112,9 @@
     limits = jnp.maximum(chosen, 0)
     groups = ((queries, limits),)
     initial = tuple((empty_states(member[0].shape[0]) for member in groups))
-    kv_piece = lax.all_gather(blended, "seq", axis=0, tiled=True)
+    kv_piece = jnp.concatenate(
+        lax.all_to_all(jnp.stack([blended] * lax.axis_size("seq")), "seq", 0, 0), axis=0
+    )
     first_row = jnp.int32(0)
     finished = tuple(
         (

time: 373 us -> 665 us (1.78)
  the two profiles are of different devices: /device:TPU:1 before, /device:TPU:87 now
where the time goes in v1:
time: 665 us; the launch traced here: 664 us
  waiting for transfers between devices  539 us (81%)
  matrix products  51.2 us (8%)
  other arithmetic  29.8 us (4%)
  local copies, waits for them, and re-layouts  25.3 us (4%)
  starting transfers between devices  17.3 us (3%)
    all_to_all x1, waiting for transfers between devices, on_device(): lax.all_to_all(jnp.stack([blended] * lax.axis_size('seq')), 'seq', 0, 0)  486 us
    all_to_all x1, waiting for transfers between devices, on_device(): lax.all_to_all(store_kv, 'store', split_axis=0, concat_axis=0, tiled=True)  52.8 us
    dot_general x1, matrix products, update(): jnp.einsum('hgqk,khd->hgqd', weights.astype(jnp.bfloat16), value_rows, pr...  27 us
    dot_general x1, matrix products, update(): jnp.einsum('qhgd,khd->hgqk', grouped, key_rows, preferred_element_type=jn...  23.6 us
    reduce_sum x1, other arithmetic, update(): running_sum = jnp.sum(weights, axis=3)  21.6 us
  transfers between devices with their start and end apart: 2, of which 2 were waited for; matrix products, arithmetic and copies ran while one was open for 1% of the time, Pallas kernels for 0%

profile of v1, /device:TPU:87, one launch (start us, length us, event | category | flops | bytes accessed | tf_op | source)
XLA Modules:
  0.0 664.4 jit_solution(1468505054324442799)
XLA Ops:
  0.7 7.6 %all-to-all-start = ((bf16[16,40,2048]{2,1,0:T(8,128)(2,1)}), bf16[16,40,2048]{2,1,0:T(8,128)(2,1)S(1)}, u32[]{:S(2)}, u32[]{:S(2)}) async-start(bf16[16,40,2048]{2,1,0:T(8,128)(2,1)} %param.8), calls=%async_computation | async-start | bytes 5242880 | tf_op jit(solution)/shard_map/all_to_all | solution.py:95
  8.2 0.7 constant_dynamic-slice_fusion
  8.9 0.3 reduce-window.9
  9.3 0.7 dynamic-slice_bitcast_fusion
  10.1 0.1 slice_reduce_fusion
  10.4 0.1 select_reduce_fusion
  10.6 0.7 compare_reduce_fusion
  11.4 0.5 multiply_cosine_fusion
  11.9 52.8 %all-to-all-done = bf16[16,40,2048]{2,1,0:T(8,128)(2,1)S(1)} async-done(((bf16[16,40,2048]{2,1,0:T(8,128)(2,1)}), bf16[16,40,2048]{2,1,0:T(8,128)(2,1)S(1)}, u32[]{:S(2)}, u32[]{:S(2)}) %all-to-all-start) | async-done | bytes 2621472 | tf_op jit(solution)/shard_map/all_to_all | solution.py:95
  64.8 2.3 gather_fusion
  67.1 1.4 select_convert_fusion
  68.7 0.2 copy.36
  68.9 0.5 multiply_subtract_fusion
  69.4 0.3 pad_maximum_fusion
  69.9 0.5 fusion.12
  70.4 0.5 copy.25
  70.9 6.1 stack.2
  77.0 9.7 %all-to-all-start.1 = ((bf16[16,256,2048]{1,2,0:T(8,128)(2,1)}), bf16[16,256,2048]{1,2,0:T(8,128)(2,1)}, u32[]{:S(2)}, u32[]{:S(2)}) async-start(bf16[16,256,2048]{1,2,0:T(8,128)(2,1)} %stack.2), calls=%async_computation.1 | async-start | bytes 33554432 | tf_op jit(solution)/shard_map/all_to_all | solution.py:116
  86.8 0.6 broadcast_maximum_fusion.2
  88.1 486.4 %all-to-all-done.1 = bf16[16,256,2048]{1,2,0:T(8,128)(2,1)} async-done(((bf16[16,256,2048]{1,2,0:T(8,128)(2,1)}), bf16[16,256,2048]{1,2,0:T(8,128)(2,1)}, u32[]{:S(2)}, u32[]{:S(2)}) %all-to-all-start.1) | async-done | bytes 16777248 | tf_op jit(solution)/shard_map/all_to_all | solution.py:116
  574.5 85.6 %conditional.1 = (f32[8,8,64]{2,1,0:T(8,128)S(1)}, f32[8,8,64,128]{3,2,1,0:T(8,128)}) conditional(s32[]{:T(128)} %convert_element_type.44, () %tuple.16, (s32[64]{0:T(128)S(1)}, bf16[16,256,2048]{1,2,0:T(8,128)(2,1)}, bf16[1,64,8192]{2,1,0:T(8,128)(2,1)}) %tuple.17), branch_computations={%region_7.8_spmd, %region_8.11_spmd} | conditional | flops 8774742016 | bytes 295797056 | solution.py:82
  574.5 0.2 iota_compare_fusion
  574.7 8.5 %copy.34 = bf16[16,256,8,256]{3,2,0,1:T(8,128)(2,1)S(1)} copy(bf16[16,256,8,256]{3,2,1,0:T(8,128)(2,1)} %bitcast.23) | data formatting | bytes 33554432 | tf_op jit(solution)/shard_map/reshape | solution.py:115
  583.2 4.3 fusion.19
  587.5 0.3 copy.35
  587.8 23.6 %fusion = (f32[8,8,64]{2,1,0:T(8,128)S(1)}, f32[8,4096,64,8]{1,2,3,0:T(8,128)}) fusion(pred[64,4096]{1,0:T(8,128)(4,1)S(1)} %iota_compare_fusion, bf16[4096,8,128,1]{0,2,3,1:T(8,128)(2,1)S(1)} %bitcast.65, bf16[64,8,8,128]{3,2,1,0:T(8,128)(2,1)S(1)} %bitcast.68), kind=kOutput, calls=%fused_computation.3 | convolution fusion | flops 4345294848 | bytes 76824576 | tf_op jit(solution)/shard_map/cond/branch_1_fun/qhgd,khd->hgqk/dot_general | solution.py:64
  611.4 27.0 %fusion.5 = f32[8,8,64,128]{3,2,1,0:T(8,128)} fusion(bf16[4096,8,128,1]{0,2,3,1:T(8,128)(2,1)} %bitcast.67, f32[8,4096,64,8]{1,2,3,0:T(8,128)} %get-tuple-element.31, f32[8,8,64]{2,1,0:T(8,128)S(1)} %broadcast_maximum_fusion, pred[64,4096]{1,0:T(8,128)(4,1)S(1)} %iota_compare_fusion), kind=kOutput, calls=%fused_computation.8 | convolution fusion | flops 4362076160 | bytes 77873152 | tf_op jit(solution)/shard_map/cond/branch_1_fun/hgqk,khd->hgqd/dot_general | solution.py:73
  638.4 21.6 %fusion.4 = f32[8,8,64]{2,1,0:T(8,128)S(1)} fusion(f32[8,4096,64,8]{1,2,3,0:T(8,128)} %get-tuple-element.31, f32[8,8,64]{2,1,0:T(8,128)S(1)} %broadcast_maximum_fusion, pred[64,4096]{1,0:T(8,128)(4,1)S(1)} %iota_compare_fusion), kind=kLoop, calls=%fused_computation.7 | loop fusion | flops 67104768 | bytes 67403776 | tf_op jit(solution)/shard_map/cond/branch_1_fun/reduce_sum | solution.py:72
  660.1 2.0 fusion.13
  662.1 0.7 copy.27
  662.8 0.5 convert_element_type.47
  663.3 1.1 broadcast_select_fusion
  (31 shorter events, 0.8 us)
Async XLA Ops:
  0.6 69.2 %copy-start = (bf16[1,64,2048]{2,1,0:T(8,128)(2,1)S(1)}, bf16[1,64,2048]{2,1,0:T(8,128)(2,1)}, u32[]{:S(2)}) copy-start(bf16[1,64,2048]{2,1,0:T(8,128)(2,1)} %param.12) | copy-start | bytes 786436
  0.6 69.2 %copy-start.4 = (s32[1,64]{1,0:T(1,128)S(1)}, s32[1,64]{1,0:T(1,128)}, u32[]{:S(2)}) copy-start(s32[1,64]{1,0:T(1,128)} %param.13) | copy-start | bytes 772
  0.7 64.1 %all-to-all-start = ((bf16[16,40,2048]{2,1,0:T(8,128)(2,1)}), bf16[16,40,2048]{2,1,0:T(8,128)(2,1)S(1)}, u32[]{:S(2)}, u32[]{:S(2)}) async-start(bf16[16,40,2048]{2,1,0:T(8,128)(2,1)} %param.8), calls=%async_computation | async-start | bytes 5242880 | tf_op jit(solution)/shard_map/all_to_all | solution.py:95
  70.4 6.6 copy-start.3
  77.0 497.5 %all-to-all-start.1 = ((bf16[16,256,2048]{1,2,0:T(8,128)(2,1)}), bf16[16,256,2048]{1,2,0:T(8,128)(2,1)}, u32[]{:S(2)}, u32[]{:S(2)}) async-start(bf16[16,256,2048]{1,2,0:T(8,128)(2,1)} %stack.2), calls=%async_computation.1 | async-start | bytes 33554432 | tf_op jit(solution)/shard_map/all_to_all | solution.py:116
  583.2 4.3 copy-start.2
  660.1 4.3 copy-start.1
